TPU v7x, 32 devices: a whole 2x2x4 slice. The times are simulated.
32 devices in a mesh: gx: 2 (over core), gy: 4 (over y, x), gz: 4 (over z).
Axes of the slice: x: 2, y: 2, z: 4, core: 2. Of those that a mesh axis runs over, the one named last changes fastest.
Arguments:
- block_values: bfloat16 [4, 64, 4, 6, 128, 128], P('gy', 'gx', 'gz'), as said below
- block_cols: int32 [4, 64, 4, 6], P('gy', 'gx', 'gz'), may hold values from 0 to 63, as said below
Outputs:
- purified: float32 [256, 32768], P(('gx', 'gy'), 'gz')
Inputs may be any that keep to these rules, and one draw needn't show every extreme that they name: block_cols[a, s, b, :] holds 6 distinct tile columns of panel b at which tile row a * 64 + s of P is nonzero; every tile column of a panel is listed by exactly 6 tile rows of each slab; the pattern is symmetric: tile (i, j) is listed exactly when tile (j, i) is. `block_values`: P is symmetric: the tile listed at (i, j) is the transpose of the tile listed at (j, i), and diagonal tiles are symmetric.
All inputs are finite; a program needn't handle non-finite values.
Results may differ from a plain program's by a relative error of at most 0.0033.
Values may be sent and summed in bfloat16 or wider, within the bound.
A program may use at most 128 MiB of HBM per device.

v0:
```python
import jax
import jax.numpy as jnp
from jax import lax
from jax.sharding import PartitionSpec as P

WIN = 1


def broadcast(value, axis, source):
    kept = jnp.where(lax.axis_index(axis) == source, value, 0).astype(value.dtype)
    return lax.psum(kept, axis)


def densify(left_tiles, left_columns, slab_tiles):
    onehot = (
        left_columns[:, :, None] == jnp.arange(slab_tiles, dtype=jnp.int32)[None, None, :]
    ).astype(jnp.bfloat16)
    densified = jnp.einsum("wkj,wkyx->wyjx", onehot, left_tiles, preferred_element_type=jnp.float32)
    tile_size = left_tiles.shape[2]
    return densified.astype(jnp.bfloat16).reshape(
        left_tiles.shape[0] * tile_size, slab_tiles, tile_size
    )


def product_one(left_panel, panel_tiles, panel_columns):
    summed = jnp.zeros(
        (left_panel.shape[0], panel_tiles.shape[0], panel_tiles.shape[2]), jnp.float32
    )
    for column_slot in range(panel_tiles.shape[1]):
        picked = jnp.take(left_panel, panel_columns[:, column_slot], axis=1)
        summed = summed + jnp.einsum(
            "rix,iyx->riy", picked, panel_tiles[:, column_slot], preferred_element_type=jnp.float32
        )
    return summed


def product_two(rounded, panel_tiles, panel_columns, panel_width):
    summed = jnp.zeros((rounded.shape[0], panel_width, panel_tiles.shape[3]), jnp.float32)
    for column_slot in range(panel_tiles.shape[1]):
        product = jnp.einsum(
            "rix,ixy->riy", rounded, panel_tiles[:, column_slot], preferred_element_type=jnp.float32
        )
        summed = summed.at[:, panel_columns[:, column_slot], :].add(product)
    return summed


def local(block_values, block_cols):
    tiles_here = block_values[0, :, 0]
    columns_here = block_cols[0, :, 0]
    tile_size = tiles_here.shape[2]
    slab_tiles = tiles_here.shape[0] * lax.axis_size("gx")
    left_tiles, left_columns = (
        broadcast(tiles_here[:WIN], "gy", 0),
        broadcast(columns_here[:WIN], "gy", 0),
    )
    left_panel = densify(left_tiles, left_columns, slab_tiles)
    height = left_panel.shape[0]
    on_diagonal = (lax.axis_index("gy") == lax.axis_index("gz")).astype(jnp.float32)
    panel_tiles, panel_columns = (
        lax.all_gather(tiles_here, "gx", axis=0, tiled=True),
        lax.all_gather(columns_here, "gx", axis=0, tiled=True),
    )
    partial_square = product_one(left_panel, panel_tiles, panel_columns)
    partial_square = partial_square.reshape(height, slab_tiles * tile_size)
    square = lax.psum(partial_square, "gz")
    square_low = square.astype(jnp.bfloat16).reshape(height, slab_tiles, tile_size)
    applied = product_two(square_low, panel_tiles, panel_columns, slab_tiles).reshape(
        lax.axis_size("gy") * (height // lax.axis_size("gy")), slab_tiles * tile_size
    )
    return lax.psum_scatter(
        3.0 * on_diagonal * square - 2.0 * applied, "gy", scatter_dimension=0, tiled=True
    )


def solution(mesh):
    in_specs = (P("gy", "gx", "gz", None, None, None), P("gy", "gx", "gz", None))
    out_specs = P(("gx", "gy"), "gz")
    return jax.shard_map(local, mesh=mesh, in_specs=in_specs, out_specs=out_specs, check_vma=False)
```

profile of v0, /device:TPU:0, one launch (start us, length us, event | category | flops | bytes accessed | tf_op | source)
XLA Modules:
  0.0 449.8 jit_solution(1277576746980991775)
XLA Ops:
  9.2 8.0 %copy.48 = bf16[1,32,1,6,128,128]{5,4,1,3,2,0:T(8,128)(2,1)} copy(bf16[1,32,1,6,128,128]{5,4,3,2,1,0:T(8,128)(2,1)} %param.4) | data formatting | bytes 12582912 | tf_op args[0]
  18.2 8.9 %psum.25 = s32[6]{0:T(128)S(1)} all-reduce(s32[6]{0:T(128)S(1)} %fusion.44), channel_id=1, replica_groups=mesh['gx'=2,'gy'=4,'gz'=4] {'gy'}, use_global_device_ids=true, to_apply=%region_1.2 | all-reduce | flops 6 | bytes 48 | tf_op jit(solution)/shard_map/psum | solution.py:11
  29.5 27.4 %all-reduce.3.cloned.1.call-done = bf16[6,128,128]{2,0,1:T(8,128)(2,1)} async-done(((bf16[6,128,128]{2,0,1:T(8,128)(2,1)}), bf16[6,128,128]{2,0,1:T(8,128)(2,1)}) %all-reduce.3.cloned.1.call-update) | async-done | bytes 196624 | tf_op jit(solution)/shard_map/psum | solution.py:11
  60.0 2.2 gather_fusion.4
  64.4 2.2 gather_fusion.2
  68.7 2.2 gather_fusion
  73.0 6.2 %fusion.1 = f32[64,128,128]{1,2,0:T(8,128)} fusion(bf16[64,128,128]{2,1,0:T(8,128)(2,1)} %gather_fusion.4, pred[64]{0:T(512)(128)(4,1)S(1)} %get-tuple-element.24, bf16[64,6,128,128]{3,2,0,1:T(8,128)(2,1)} %bitcast.77), kind=kOutput, calls=%fused_computation.21 | convolution fusion | flops 269484032 | bytes 8388672 | tf_op jit(solution)/shard_map/rix,iyx->riy/dot_general | solution.py:31
  79.1 6.0 %fusion.3 = f32[64,128,128]{1,2,0:T(8,128)} fusion(bf16[64,128,128]{2,1,0:T(8,128)(2,1)} %gather_fusion.3, pred[64]{0:T(512)(128)(4,1)S(1)} %get-tuple-element.25, bf16[64,6,128,128]{3,2,0,1:T(8,128)(2,1)} %bitcast.78), kind=kOutput, calls=%fused_computation.23 | convolution fusion | flops 269484032 | bytes 8388672 | tf_op jit(solution)/shard_map/rix,iyx->riy/dot_general | solution.py:31
  85.2 3.6 fusion.5
  88.8 3.6 fusion.7
  92.4 3.6 fusion.9
  96.0 10.1 %add_add_fusion = f32[64,128,128]{1,2,0:T(8,128)} fusion(f32[64,128,128]{1,2,0:T(8,128)} %fusion.1, f32[64,128,128]{1,2,0:T(8,128)} %fusion.3, f32[64,128,128]{1,2,0:T(8,128)} %fusion.5, f32[64,128,128]{1,2,0:T(8,128)} %fusion.9, f32[64,128,128]{1,2,0:T(8,128)} %fusion.7, bf16[64,128,128]{2,1,0:T(8,128)(2,1)S(1)} %copy-done.4, ...), kind=kOutput, calls=%fused_computation.13 | convolution fusion | flops 274726912 | bytes 29360640 | tf_op jit(solution)/shard_map/rix,iyx->riy/dot_general | solution.py:31
  106.4 154.9 %all-reduce.5.cloned.1.call-done = f32[128,8192]{0,1:T(8,128)} async-done(((f32[128,8192]{0,1:T(8,128)}), f32[128,8192]{0,1:T(8,128)}) %all-reduce.5.cloned.1.call-update) | async-done | bytes 4194320 | tf_op jit(solution)/shard_map/psum | solution.py:65
  261.3 2.5 convert_element_type.19
  263.8 4.5 %fusion.24 = f32[64,128,128]{2,1,0:T(8,128)} fusion(bf16[128,64,128]{0,2,1:T(8,128)(2,1)S(1)} %bitcast.71, bf16[64,6,128,128]{3,2,0,1:T(8,128)(2,1)} %bitcast.79), kind=kOutput, calls=%fused_computation.46 | convolution fusion | flops 268435456 | bytes 8388608 | tf_op jit(solution)/shard_map/rix,ixy->riy/dot_general | solution.py:40
  268.4 4.6 %fusion.23 = f32[64,128,128]{2,1,0:T(8,128)} fusion(bf16[128,64,128]{0,2,1:T(8,128)(2,1)S(1)} %bitcast.72, bf16[64,6,128,128]{3,2,0,1:T(8,128)(2,1)} %bitcast.80), kind=kOutput, calls=%fused_computation.45 | convolution fusion | flops 268435456 | bytes 8388608 | tf_op jit(solution)/shard_map/rix,ixy->riy/dot_general | solution.py:40
  272.9 2.8 fusion.25
  275.8 2.8 fusion.26
  278.6 2.8 fusion.27
  281.4 2.8 fusion.28
  284.2 2.5 broadcast_in_dim.30
  286.7 13.9 %scatter_fusion = f32[128,64,128]{2,0,1:T(8,128)} fusion(f32[128,64,128]{2,0,1:T(8,128)} %broadcast_in_dim.30, s32[64]{0:T(128)S(1)} %get-tuple-element.7, f32[64,128,128]{2,1,0:T(8,128)} %fusion.23), kind=kCustom, calls=%fused_computation.6 | custom fusion | flops 1048576 | bytes 12583168 | tf_op jit(solution)/shard_map/scatter-add | solution.py:43
  300.6 13.6 %scatter_fusion.1 = f32[128,64,128]{2,0,1:T(8,128)} fusion(f32[128,64,128]{2,0,1:T(8,128)} %scatter_fusion, s32[64]{0:T(128)S(1)} %get-tuple-element.8, f32[64,128,128]{2,1,0:T(8,128)} %fusion.24), kind=kCustom, calls=%fused_computation.7 | custom fusion | flops 1048576 | bytes 12583168 | tf_op jit(solution)/shard_map/scatter-add | solution.py:43
  314.2 13.6 %scatter_fusion.2 = f32[128,64,128]{2,0,1:T(8,128)} fusion(f32[128,64,128]{2,0,1:T(8,128)} %scatter_fusion.1, s32[64]{0:T(128)S(1)} %get-tuple-element.9, f32[64,128,128]{2,1,0:T(8,128)} %fusion.25), kind=kCustom, calls=%fused_computation.8 | custom fusion | flops 1048576 | bytes 12583168 | tf_op jit(solution)/shard_map/scatter-add | solution.py:43
  327.9 13.7 %scatter_fusion.3 = f32[128,64,128]{2,0,1:T(8,128)} fusion(f32[128,64,128]{2,0,1:T(8,128)} %scatter_fusion.2, s32[64]{0:T(128)S(1)} %get-tuple-element.10, f32[64,128,128]{2,1,0:T(8,128)} %fusion.26), kind=kCustom, calls=%fused_computation.9 | custom fusion | flops 1048576 | bytes 12583168 | tf_op jit(solution)/shard_map/scatter-add | solution.py:43
  341.6 13.7 %scatter_fusion.4 = f32[128,64,128]{2,0,1:T(8,128)} fusion(f32[128,64,128]{2,0,1:T(8,128)} %scatter_fusion.3, s32[64]{0:T(128)S(1)} %get-tuple-element.11, f32[64,128,128]{2,1,0:T(8,128)} %fusion.27), kind=kCustom, calls=%fused_computation.10 | custom fusion | flops 1048576 | bytes 12583168 | tf_op jit(solution)/shard_map/scatter-add | solution.py:43
  355.2 13.6 %scatter_fusion.5 = f32[128,64,128]{2,0,1:T(8,128)} fusion(f32[128,64,128]{2,0,1:T(8,128)} %scatter_fusion.4, s32[64]{0:T(128)S(1)} %get-tuple-element.6, f32[64,128,128]{2,1,0:T(8,128)} %fusion.28), kind=kCustom, calls=%fused_computation.11 | custom fusion | flops 1048576 | bytes 12583168 | tf_op jit(solution)/shard_map/scatter-add | solution.py:43
  368.9 4.7 %broadcast_multiply_fusion = f32[128,64,128]{2,0,1:T(8,128)} fusion(f32[128,64,128]{2,0,1:T(8,128)} %scatter_fusion.5), kind=kLoop, calls=%fused_computation.37 | loop fusion | flops 1048576 | bytes 8388608 | tf_op jit(solution)/shard_map/mul | solution.py:71
  373.6 5.6 %copy.60 = f32[128,64,128]{0,2,1:T(8,128)} copy(f32[128,64,128]{2,0,1:T(8,128)} %broadcast_multiply_fusion) | data formatting | bytes 8388608 | tf_op jit(solution)/shard_map/mul | solution.py:71
  379.2 5.8 %bitcast_subtract_fusion = f32[128,8192]{0,1:T(8,128)} fusion(f32[128,64,128]{0,2,1:T(8,128)} %copy.60, f32[128,8192]{0,1:T(8,128)} %all-reduce.5.cloned.1.call-done, f32[]{:T(128)S(6)} %mul_shard_map.3), kind=kLoop, calls=%fused_computation.12 | loop fusion | flops 2097152 | bytes 12582916 | tf_op jit(solution)/shard_map/sub | solution.py:71
  385.1 5.6 %copy.68 = f32[128,8192]{1,0:T(8,128)} copy(f32[128,8192]{0,1:T(8,128)} %bitcast_subtract_fusion) | data formatting | bytes 8388608
  390.7 51.9 %reduce-scatter.4.cloned.1.call-done = f32[32,8192]{1,0:T(8,128)} async-done(((f32[128,8192]{1,0:T(8,128)}), f32[32,8192]{1,0:T(8,128)}) %reduce-scatter.4.cloned.1.call-update) | async-done | bytes 1048592 | tf_op jit(solution)/shard_map/reduce_scatter | solution.py:70
  (52 shorter events, 14.9 us)
Async XLA Ops:
  7.4 49.5 %all-reduce.3.cloned.1.call-start = ((), (), s32[]{:S(2)}) async-start(), calls=%async_computation.1 | async-start | bytes 524288 | tf_op jit(solution)/shard_map/psum | solution.py:11
  9.2 63.8 %all-gather.4.cloned.1.call-start = ((), (), s32[]{:S(2)}) async-start(), calls=%async_computation.3 | async-start | bytes 18874368 | tf_op jit(solution)/shard_map/all_gather | solution.py:60
  17.3 0.7 copy-start.5
  17.3 244.0 %all-reduce.5.cloned.1.call-start = ((), (), s32[]{:S(2)}) async-start(), calls=%async_computation.2 | async-start | bytes 8388608 | tf_op jit(solution)/shard_map/psum | solution.py:65
  73.0 12.2 %copy-start = (bf16[1,64,1,6,128,128]{5,4,1,3,2,0:T(8,128)(2,1)S(1)}, bf16[1,64,1,6,128,128]{5,4,1,3,2,0:T(8,128)(2,1)}, u32[]{:S(2)}) copy-start(bf16[1,64,1,6,128,128]{5,4,1,3,2,0:T(8,128)(2,1)} %all-gather.4.cloned.1.call-done) | copy-start | bytes 37748740
  79.1 6.0 %copy-start.3 = (bf16[64,128,128]{2,1,0:T(8,128)(2,1)S(1)}, bf16[64,128,128]{2,1,0:T(8,128)(2,1)}, u32[]{:S(2)}) copy-start(bf16[64,128,128]{2,1,0:T(8,128)(2,1)} %gather_fusion.2) | copy-start | bytes 6291460
  85.2 3.6 copy-start.2
  88.8 3.6 copy-start.1
  92.4 3.6 copy-start.4
  106.1 336.5 %reduce-scatter.4.cloned.1.call-start = ((), (), s32[]{:S(2)}) async-start(), calls=%async_computation.4 | async-start | bytes 5242880 | tf_op jit(solution)/shard_map/reduce_scatter | solution.py:70
  261.3 11.7 %slice-start = ((s8[12582912]{0:T(1024)(128)(4,1)}), s8[4194304]{0:T(1024)(128)(4,1)S(1)}, s32[]{:S(2)}) async-start(s8[12582912]{0:T(1024)(128)(4,1)} %bitcast.85), calls=%async_computation.5 | async-start | bytes 8388608
  263.8 9.1 %slice-start.1 = ((s8[12582912]{0:T(1024)(128)(4,1)}), s8[4194304]{0:T(1024)(128)(4,1)S(1)}, s32[]{:S(2)}) async-start(s8[12582912]{0:T(1024)(128)(4,1)} %bitcast.85), calls=%async_computation.6 | async-start | bytes 8388608
  268.3 4.6 %slice-start.2 = ((s8[12582912]{0:T(1024)(128)(4,1)}), s8[4194304]{0:T(1024)(128)(4,1)S(1)}, s32[]{:S(2)}) async-start(s8[12582912]{0:T(1024)(128)(4,1)} %bitcast.85), calls=%async_computation.7 | async-start | bytes 8388608
Sparse Core Ops, SparseCore 0:
  11.1 45.7 all-reduce.2
  106.3 154.9 all-reduce.4
  390.8 51.7 reduce-scatter.3
Sparse Core Ops, SparseCore 1:
  17.4 27.3 all-gather.3
where the time goes:
time: 451 us; the launch traced here: 450 us
  waiting for transfers between devices  234 us (52%)
  other arithmetic  96.8 us (21%)
  matrix products  55.3 us (12%)
  local copies, waits for them, and re-layouts  37.7 us (8%)
  between operations  14.7 us (3%)
  blocking collectives  10.7 us (2%)
    psum x1, waiting for transfers between devices, local(): square = lax.psum(partial_square, 'gz')  155 us
    scatter-add x6, other arithmetic, product_two(): summed = summed.at[:, panel_columns[:, column_slot], :].add(product)  82.2 us
    reduce_scatter x1, waiting for transfers between devices, local(): lax.psum_scatter(3.0 * on_diagonal * square - 2.0 * applied, 'gy', scatte...  51.9 us
    dot_general x6, matrix products, product_one(): jnp.einsum('rix,iyx->riy', picked, panel_tiles[:, column_slot], preferred...  33.1 us
    psum x1, waiting for transfers between devices, broadcast(): return lax.psum(kept, axis)  27.4 us
    dot_general x6, matrix products, product_two(): jnp.einsum('rix,ixy->riy', rounded, panel_tiles[:, column_slot], preferre...  20.4 us
    unnamed x21, local copies, waits for them, and re-layouts  14.4 us
    gather x6, local copies, waits for them, and re-layouts, product_one(): picked = jnp.take(left_panel, panel_columns[:, column_slot], axis=1)  12.9 us
  transfers between devices with their start and end apart: 4, of which 3 were waited for; matrix products, arithmetic and copies ran while one was open for 6% of the time, Pallas kernels for 0%

commit v1 on v0

--- a/solution.py
+++ b/solution.py
@@ -4,6 +4,15 @@
 from jax.sharding import PartitionSpec as P
 
 WIN = 1
+
+
+def doubling_sum(value, name):
+    peers = lax.axis_size(name)
+    summed, hop = (value, 1)
+    while hop < peers:
+        summed = summed + lax.ppermute(summed, name, [(i, i ^ hop) for i in range(peers)])
+        hop = 2 * hop
+    return summed
 
 
 def broadcast(value, axis, source):
@@ -62,7 +71,7 @@
     )
     partial_square = product_one(left_panel, panel_tiles, panel_columns)
     partial_square = partial_square.reshape(height, slab_tiles * tile_size)
-    square = lax.psum(partial_square, "gz")
+    square = doubling_sum(partial_square, "gz")
     square_low = square.astype(jnp.bfloat16).reshape(height, slab_tiles, tile_size)
     applied = product_two(square_low, panel_tiles, panel_columns, slab_tiles).reshape(
         lax.axis_size("gy") * (height // lax.axis_size("gy")), slab_tiles * tile_size

time: 451 us -> 579 us (1.28)
  waiting for transfers between devices: 234 us -> 351 us
  other arithmetic: 96.8 us -> 104 us
    ppermute x0 -> x2, waiting for transfers between devices: none -> 270 us  [doubling_sum(): lax.ppermute(summed, name, [(i, i ^ hop) for i in range(peers)])]
    psum x1 -> x0, waiting for transfers between devices: 155 us -> none  [local(): square = lax.psum(partial_square, 'gz')]
  transfers between devices with their start and end apart: 4 -> 5, of which waited for: 3 -> 4; matrix products, arithmetic and copies ran while one was open for 6% -> 4% of each run, Pallas kernels for 0% -> 0%
where the time goes in v1:
time: 579 us; the launch traced here: 578 us
  waiting for transfers between devices  351 us (61%)
  other arithmetic  104 us (18%)
  matrix products  55.8 us (10%)
  local copies, waits for them, and re-layouts  37.8 us (7%)
  between operations  15 us (3%)
  blocking collectives  10.7 us (2%)
    ppermute x2, waiting for transfers between devices, doubling_sum(): lax.ppermute(summed, name, [(i, i ^ hop) for i in range(peers)])  270 us
    scatter-add x6, other arithmetic, product_two(): summed = summed.at[:, panel_columns[:, column_slot], :].add(product)  82.1 us
    reduce_scatter x1, waiting for transfers between devices, local(): lax.psum_scatter(3.0 * on_diagonal * square - 2.0 * applied, 'gy', scatte...  52.9 us
    dot_general x6, matrix products, product_one(): jnp.einsum('rix,iyx->riy', picked, panel_tiles[:, column_slot], preferred...  33.1 us
    psum x1, waiting for transfers between devices, broadcast(): return lax.psum(kept, axis)  27.4 us
    dot_general x6, matrix products, product_two(): jnp.einsum('rix,ixy->riy', rounded, panel_tiles[:, column_slot], preferre...  20.9 us
    unnamed x21, local copies, waits for them, and re-layouts  14.4 us
    gather x6, local copies, waits for them, and re-layouts, product_one(): picked = jnp.take(left_panel, panel_columns[:, column_slot], axis=1)  12.9 us
  transfers between devices with their start and end apart: 5, of which 4 were waited for; matrix products, arithmetic and copies ran while one was open for 4% of the time, Pallas kernels for 0%

profile of v1, /device:TPU:0, one launch (start us, length us, event | category | flops | bytes accessed | tf_op | source)
XLA Modules:
  0.0 578.1 jit_solution(13406000915250763816)
XLA Ops:
  9.2 8.0 %copy.55 = bf16[1,32,1,6,128,128]{5,4,1,3,2,0:T(8,128)(2,1)} copy(bf16[1,32,1,6,128,128]{5,4,3,2,1,0:T(8,128)(2,1)} %param.4) | data formatting | bytes 12582912 | tf_op args[0]
  18.2 8.9 %psum.18 = s32[6]{0:T(128)S(1)} all-reduce(s32[6]{0:T(128)S(1)} %fusion.44), channel_id=1, replica_groups=mesh['gx'=2,'gy'=4,'gz'=4] {'gy'}, use_global_device_ids=true, to_apply=%region_1.2 | all-reduce | flops 6 | bytes 48 | tf_op jit(solution)/shard_map/psum | solution.py:20
  29.5 27.4 %all-reduce.2.cloned.1.call-done = bf16[6,128,128]{2,0,1:T(8,128)(2,1)} async-done(((bf16[6,128,128]{2,0,1:T(8,128)(2,1)}), bf16[6,128,128]{2,0,1:T(8,128)(2,1)}) %all-reduce.2.cloned.1.call-update) | async-done | bytes 196624 | tf_op jit(solution)/shard_map/psum | solution.py:20
  73.0 6.2 %fusion.1 = f32[64,128,128]{1,2,0:T(8,128)} fusion(bf16[64,128,128]{2,1,0:T(8,128)(2,1)} %gather_fusion.4, pred[64]{0:T(512)(128)(4,1)S(1)} %get-tuple-element.24, bf16[64,6,128,128]{3,2,0,1:T(8,128)(2,1)} %bitcast.78), kind=kOutput, calls=%fused_computation.21 | convolution fusion | flops 269484032 | bytes 8388672 | tf_op jit(solution)/shard_map/rix,iyx->riy/dot_general | solution.py:40
  79.1 6.0 %fusion.3 = f32[64,128,128]{1,2,0:T(8,128)} fusion(bf16[64,128,128]{2,1,0:T(8,128)(2,1)} %gather_fusion.3, pred[64]{0:T(512)(128)(4,1)S(1)} %get-tuple-element.25, bf16[64,6,128,128]{3,2,0,1:T(8,128)(2,1)} %bitcast.79), kind=kOutput, calls=%fused_computation.23 | convolution fusion | flops 269484032 | bytes 8388672 | tf_op jit(solution)/shard_map/rix,iyx->riy/dot_general | solution.py:40
  85.2 3.6 fusion.5
  88.8 3.6 fusion.7
  92.4 3.6 fusion.9
  96.0 10.1 %add_add_fusion = f32[64,128,128]{1,2,0:T(8,128)} fusion(f32[64,128,128]{1,2,0:T(8,128)} %fusion.1, f32[64,128,128]{1,2,0:T(8,128)} %fusion.3, f32[64,128,128]{1,2,0:T(8,128)} %fusion.5, f32[64,128,128]{1,2,0:T(8,128)} %fusion.9, f32[64,128,128]{1,2,0:T(8,128)} %fusion.7, bf16[64,128,128]{2,1,0:T(8,128)(2,1)S(1)} %copy-done.4, ...), kind=kOutput, calls=%fused_computation.13 | convolution fusion | flops 274726912 | bytes 29360640 | tf_op jit(solution)/shard_map/rix,iyx->riy/dot_general | solution.py:40
  107.6 90.6 %collective-permute-done = f32[128,8192]{0,1:T(8,128)S(1)} collective-permute-done((f32[128,8192]{0,1:T(8,128)}, f32[128,8192]{0,1:T(8,128)S(1)}, u32[]{:S(2)}, u32[]{:S(2)}) %collective-permute-start) | collective-permute-done | bytes 4194336 | tf_op jit(solution)/shard_map/ppermute | solution.py:13
  198.2 4.7 bitcast_add_fusion
  202.9 2.4 collective-permute-start.1
  205.2 179.7 %collective-permute-done.1 = f32[128,8192]{0,1:T(8,128)} collective-permute-done((f32[128,8192]{0,1:T(8,128)}, f32[128,8192]{0,1:T(8,128)}, u32[]{:S(2)}, u32[]{:S(2)}) %collective-permute-start.1) | collective-permute-done | bytes 4194336 | tf_op jit(solution)/shard_map/ppermute | solution.py:13
  384.9 4.0 add_convert_fusion
  389.0 5.2 fusion.24
  394.2 4.4 fusion.23
  398.6 2.8 fusion.25
  401.5 2.8 fusion.26
  404.3 2.8 fusion.27
  407.1 2.8 fusion.28
  409.9 2.6 broadcast_in_dim.30
  412.5 13.7 %scatter_fusion = f32[128,64,128]{2,0,1:T(8,128)} fusion(f32[128,64,128]{2,0,1:T(8,128)} %broadcast_in_dim.30, s32[64]{0:T(128)S(1)} %get-tuple-element.7, f32[64,128,128]{2,1,0:T(8,128)} %fusion.23), kind=kCustom, calls=%fused_computation.6 | custom fusion | flops 1048576 | bytes 12583168 | tf_op jit(solution)/shard_map/scatter-add | solution.py:52
  426.2 13.6 %scatter_fusion.1 = f32[128,64,128]{2,0,1:T(8,128)} fusion(f32[128,64,128]{2,0,1:T(8,128)} %scatter_fusion, s32[64]{0:T(128)S(1)} %get-tuple-element.8, f32[64,128,128]{2,1,0:T(8,128)} %fusion.24), kind=kCustom, calls=%fused_computation.7 | custom fusion | flops 1048576 | bytes 12583168 | tf_op jit(solution)/shard_map/scatter-add | solution.py:52
  439.8 13.6 %scatter_fusion.2 = f32[128,64,128]{2,0,1:T(8,128)} fusion(f32[128,64,128]{2,0,1:T(8,128)} %scatter_fusion.1, s32[64]{0:T(128)S(1)} %get-tuple-element.9, f32[64,128,128]{2,1,0:T(8,128)} %fusion.25), kind=kCustom, calls=%fused_computation.8 | custom fusion | flops 1048576 | bytes 12583168 | tf_op jit(solution)/shard_map/scatter-add | solution.py:52
  453.4 13.6 %scatter_fusion.3 = f32[128,64,128]{2,0,1:T(8,128)} fusion(f32[128,64,128]{2,0,1:T(8,128)} %scatter_fusion.2, s32[64]{0:T(128)S(1)} %get-tuple-element.10, f32[64,128,128]{2,1,0:T(8,128)} %fusion.26), kind=kCustom, calls=%fused_computation.9 | custom fusion | flops 1048576 | bytes 12583168 | tf_op jit(solution)/shard_map/scatter-add | solution.py:52
  467.0 13.7 %scatter_fusion.4 = f32[128,64,128]{2,0,1:T(8,128)} fusion(f32[128,64,128]{2,0,1:T(8,128)} %scatter_fusion.3, s32[64]{0:T(128)S(1)} %get-tuple-element.11, f32[64,128,128]{2,1,0:T(8,128)} %fusion.27), kind=kCustom, calls=%fused_computation.10 | custom fusion | flops 1048576 | bytes 12583168 | tf_op jit(solution)/shard_map/scatter-add | solution.py:52
  480.7 13.8 %scatter_fusion.5 = f32[128,64,128]{2,0,1:T(8,128)} fusion(f32[128,64,128]{2,0,1:T(8,128)} %scatter_fusion.4, s32[64]{0:T(128)S(1)} %get-tuple-element.6, f32[64,128,128]{2,1,0:T(8,128)} %fusion.28), kind=kCustom, calls=%fused_computation.11 | custom fusion | flops 1048576 | bytes 12583168 | tf_op jit(solution)/shard_map/scatter-add | solution.py:52
  494.6 4.7 broadcast_multiply_fusion
  499.3 5.6 copy.67
  504.9 7.2 %bitcast_subtract_fusion = f32[128,8192]{0,1:T(8,128)} fusion(f32[128,64,128]{0,2,1:T(8,128)} %copy.67, f32[]{:T(128)S(6)} %mul_shard_map.3, f32[128,8192]{0,1:T(8,128)} %bitcast_add_fusion, f32[128,8192]{0,1:T(8,128)} %collective-permute-done.1), kind=kLoop, calls=%fused_computation.12 | loop fusion | flops 3145728 | bytes 16777220 | tf_op jit(solution)/shard_map/sub | solution.py:80
  512.1 5.6 copy.75
  517.8 52.9 %reduce-scatter.4.cloned.1.call-done = f32[32,8192]{1,0:T(8,128)} async-done(((f32[128,8192]{1,0:T(8,128)}), f32[32,8192]{1,0:T(8,128)}) %reduce-scatter.4.cloned.1.call-update) | async-done | bytes 1048592 | tf_op jit(solution)/shard_map/reduce_scatter | solution.py:79
  (54 shorter events, 22.7 us)
Async XLA Ops:
  7.4 49.5 %all-reduce.2.cloned.1.call-start = ((), (), s32[]{:S(2)}) async-start(), calls=%async_computation.1 | async-start | bytes 524288 | tf_op jit(solution)/shard_map/psum | solution.py:20
  9.2 63.8 %all-gather.4.cloned.1.call-start = ((), (), s32[]{:S(2)}) async-start(), calls=%async_computation.2 | async-start | bytes 18874368 | tf_op jit(solution)/shard_map/all_gather | solution.py:69
  17.3 0.7 copy-start.5
  17.3 553.4 %reduce-scatter.4.cloned.1.call-start = ((), (), s32[]{:S(2)}) async-start(), calls=%async_computation.3 | async-start | bytes 5242880 | tf_op jit(solution)/shard_map/reduce_scatter | solution.py:79
  73.0 12.2 %copy-start = (bf16[1,64,1,6,128,128]{5,4,1,3,2,0:T(8,128)(2,1)S(1)}, bf16[1,64,1,6,128,128]{5,4,1,3,2,0:T(8,128)(2,1)}, u32[]{:S(2)}) copy-start(bf16[1,64,1,6,128,128]{5,4,1,3,2,0:T(8,128)(2,1)} %all-gather.4.cloned.1.call-done) | copy-start | bytes 37748740
  79.1 6.0 %copy-start.3 = (bf16[64,128,128]{2,1,0:T(8,128)(2,1)S(1)}, bf16[64,128,128]{2,1,0:T(8,128)(2,1)}, u32[]{:S(2)}) copy-start(bf16[64,128,128]{2,1,0:T(8,128)(2,1)} %gather_fusion.2) | copy-start | bytes 6291460
  85.2 3.6 copy-start.2
  88.8 3.6 copy-start.1
  92.4 3.6 copy-start.4
  106.1 92.1 %collective-permute-start = (f32[128,8192]{0,1:T(8,128)}, f32[128,8192]{0,1:T(8,128)S(1)}, u32[]{:S(2)}, u32[]{:S(2)}) collective-permute-start(f32[128,8192]{0,1:T(8,128)} %bitcast.92), channel_id=1, source_target_pairs={{0,1},{1,0},{2,3},{3,2},{4,5},{5,4},{6,7},{7,6},{8,9},{9,8},{10,11... | collective-permute-start | bytes 12582920 | tf_op jit(solution)/shard_map/ppermute | solution.py:13
  202.9 182.1 %collective-permute-start.1 = (f32[128,8192]{0,1:T(8,128)}, f32[128,8192]{0,1:T(8,128)}, u32[]{:S(2)}, u32[]{:S(2)}) collective-permute-start(f32[128,8192]{0,1:T(8,128)} %bitcast_add_fusion), channel_id=1, source_target_pairs={{0,2},{1,3},{2,0},{3,1},{4,6},{5,7},{6,4},{7,5},{8,10},{9,11},{10,... | collective-permute-start | bytes 12582920 | tf_op jit(solution)/shard_map/ppermute | solution.py:13
  384.9 13.7 %slice-start = ((s8[12582912]{0:T(1024)(128)(4,1)}), s8[4194304]{0:T(1024)(128)(4,1)S(1)}, s32[]{:S(2)}) async-start(s8[12582912]{0:T(1024)(128)(4,1)} %bitcast.86), calls=%async_computation.4 | async-start | bytes 8388608
  384.9 13.7 %slice-start.1 = ((s8[12582912]{0:T(1024)(128)(4,1)}), s8[4194304]{0:T(1024)(128)(4,1)S(1)}, s32[]{:S(2)}) async-start(s8[12582912]{0:T(1024)(128)(4,1)} %bitcast.86), calls=%async_computation.5 | async-start | bytes 8388608
  389.0 9.7 %slice-start.2 = ((s8[12582912]{0:T(1024)(128)(4,1)}), s8[4194304]{0:T(1024)(128)(4,1)S(1)}, s32[]{:S(2)}) async-start(s8[12582912]{0:T(1024)(128)(4,1)} %bitcast.86), calls=%async_computation.6 | async-start | bytes 8388608
Sparse Core Ops, SparseCore 0:
  11.1 45.7 all-reduce.1
  517.9 52.7 reduce-scatter.3
Sparse Core Ops, SparseCore 1:
  17.4 27.3 all-gather.3
